TPU v7x, 128 devices: a whole 4x4x4 slice. The times are simulated.
128 devices in a mesh: dp: 8 (over y_lo, z), head: 16 (over x, y_hi, core).
Axes of the slice: x: 4, y: 4 (y_hi: 2, y_lo: 2; y = y_hi * 2 + y_lo), z: 4, core: 2. Of those that a mesh axis runs over, the one named last changes fastest.
Arguments:
- projected: bfloat16 [49152, 24576], P(('dp', 'head')), may hold values from -64 to 64, as said below
- weight_exp: int32 [49152], P(('dp', 'head')), may hold values from 0 to 3
- damp_exp: int32 [128], replicated, may hold values from 0 to 2
Outputs:
- whitening: float32 [128, 192, 192], P('head')
Inputs may be any that keep to these rules, and one draw needn't show every extreme that they name: `projected`: real values.
All inputs are finite; a program needn't handle non-finite values.
Results may differ from a plain program's by a relative error of at most 0.0003.
Values may be sent and summed in bfloat16 or wider, within the bound.
A program may use at most 192 MiB of HBM per device.

v0:
```python
import jax
import jax.numpy as jnp
from jax import lax
from jax.sharding import PartitionSpec as P

HD = 192


def split_up(shard, dim, length):
    before, after = (shard.shape[:dim], shard.shape[dim + 1 :])
    return jnp.moveaxis(shard.reshape(*before, length, -1, *after), dim, 0)


def sum_at_owner(shard, axis, dim):
    length = lax.axis_size(axis)
    blocks = lax.all_to_all(split_up(shard, dim, length), axis, 0, 0, tiled=True)
    return jnp.sum(blocks, axis=0)


def from_everyone(shard, axis):
    length = lax.axis_size(axis)
    return lax.all_to_all(
        jnp.broadcast_to(shard[None], (length, *shard.shape)), axis, 0, 0, tiled=True
    )


def in_order(blocks, dim):
    shape = list(blocks.shape[1:])
    shape[dim] *= blocks.shape[0]
    return jnp.moveaxis(blocks, 0, dim).reshape(shape)


def gather_directly(shard, axis, dim):
    blocks = from_everyone(shard, axis)
    return in_order(blocks, dim)


def pack_sym(full):
    size = full.shape[-1]
    half = size // 2
    upper_left = full[..., :half, :half]
    lower_right = full[..., half:, half:]
    lower_left = full[..., half:, :half]
    row_ids = lax.broadcasted_iota(jnp.int32, (half + 1, half), 0)
    col_ids = lax.broadcasted_iota(jnp.int32, (half + 1, half), 1)
    zero_row = jnp.zeros(full.shape[:-2] + (1, half), full.dtype)
    below = jnp.concatenate((zero_row, upper_left), axis=-2)
    above = jnp.concatenate((jnp.swapaxes(lower_right, -1, -2), zero_row), axis=-2)
    top = jnp.where(row_ids > col_ids, below, above)
    return jnp.concatenate((top, lower_left), axis=-2)


def unpack_sym(packed):
    half = packed.shape[-1]
    top = packed[..., : half + 1, :]
    lower_left = packed[..., half + 1 :, :]
    row_ids = lax.broadcasted_iota(jnp.int32, (half, half), 0)
    col_ids = lax.broadcasted_iota(jnp.int32, (half, half), 1)
    first_block = top[..., 1:, :]
    upper_left = jnp.where(row_ids >= col_ids, first_block, jnp.swapaxes(first_block, -1, -2))
    turned = jnp.swapaxes(top[..., :half, :], -1, -2)
    lower_right = jnp.where(row_ids >= col_ids, turned, jnp.swapaxes(turned, -1, -2))
    upper = jnp.concatenate((upper_left, jnp.swapaxes(lower_left, -1, -2)), axis=-1)
    bottom = jnp.concatenate((lower_left, lower_right), axis=-1)
    return jnp.concatenate((upper, bottom), axis=-2)


def encode(grams):
    return pack_sym(grams)


def decode(sent):
    return unpack_sym(sent)


def block_grams(rows, weighted, count):
    left = rows.reshape(rows.shape[0], count, HD)
    right = weighted.reshape(rows.shape[0], count, HD)
    return jnp.einsum("tch,tcg->chg", left, right, preferred_element_type=jnp.float32)


def whiten(grams, damp_exp, first, count):
    exponents = lax.dynamic_slice_in_dim(damp_exp, first, count, 0).astype(jnp.float32)
    size = grams.shape[-1]
    eye = jnp.eye(size, dtype=jnp.float32)
    level = jnp.trace(grams, axis1=1, axis2=2) / size + 1e-06
    damped = grams + (jnp.exp2(-exponents) * level)[:, None, None] * eye
    lower = jnp.linalg.cholesky(damped)

    def invert(factor):
        return jax.scipy.linalg.solve_triangular(factor, eye, lower=True)

    return jax.vmap(invert)(lower)


def on_device(projected, weight_exp, damp_exp):
    n_head = lax.axis_size("head")
    n_dp = lax.axis_size("dp")
    mats = projected.shape[1] // HD
    per_head = mats // n_head
    total = projected.shape[0] * n_head * n_dp
    weights = jnp.exp2(weight_exp.astype(jnp.float32)).astype(jnp.bfloat16)
    scaled = projected * weights[:, None]
    partial_grams = lax.psum_scatter(
        encode(block_grams(projected, scaled, lax.axis_size("head") * per_head) / total),
        "head",
        scatter_dimension=0,
        tiled=True,
    )
    head_base = lax.axis_index("head") * per_head
    share = per_head // n_dp
    owned = sum_at_owner(partial_grams, "dp", 0)
    first = head_base + lax.axis_index("dp") * share
    factors = whiten(decode(owned), damp_exp, first, share)
    return gather_directly(factors, "dp", 0)


def solution(mesh):
    return jax.shard_map(
        on_device,
        mesh=mesh,
        in_specs=(P(("dp", "head"), None), P(("dp", "head")), P()),
        out_specs=P("head", None, None),
        check_vma=False,
    )
```

profile of v0, /device:TPU:1, one launch (start us, length us, event | category | flops | bytes accessed | tf_op | source)
XLA Modules:
  0.0 345.9 jit_solution(16283828138328992014)
XLA Ops:
  6.5 0.0 reduce-scatter.2.cloned.1.call-start
  6.6 0.0 copy-start
  6.6 24.6 %copy.30 = bf16[384,24576]{0,1:T(8,128)(2,1)} copy(bf16[384,24576]{1,0:T(8,128)(2,1)} %param.3) | data formatting | bytes 37748736 | tf_op args[0]
  31.2 0.0 copy-done
  31.2 16.5 %broadcast_multiply_fusion = bf16[384,24576]{0,1:T(8,128)(2,1)} fusion(bf16[384,24576]{0,1:T(8,128)(2,1)} %copy.30, bf16[384]{0:T(512)(128)(2,1)S(1)} %exponential_convert_fusion), kind=kLoop, calls=%fused_computation.2 | loop fusion | flops 9437184 | bytes 37749504 | tf_op jit(solution)/shard_map/mul | solution.py:103
  47.7 23.7 %multiply_bitcast_fusion = f32[128,192,192]{1,2,0:T(8,128)} fusion(bf16[384,128,192]{0,2,1:T(8,128)(2,1)} %bitcast.81, bf16[384,128,192]{0,2,1:T(8,128)(2,1)} %bitcast.80), kind=kOutput, calls=%fused_computation | convolution fusion | flops 3628597248 | bytes 56623104 | tf_op jit(solution)/shard_map/tch,tcg->chg/dot_general | solution.py:79
  71.4 18.7 %fusion.9 = (f32[128,96,96]{1,2,0:T(8,128)}, f32[128,96,96]{1,2,0:T(8,128)}, f32[128,96,96]{2,1,0:T(8,128)}) fusion(f32[128,192,192]{1,2,0:T(8,128)} %multiply_bitcast_fusion), kind=kLoop, calls=%fused_computation.54 | loop fusion | bytes 28311552 | tf_op jit(solution)/shard_map/slice | solution.py:41
  90.1 6.6 %copy.48 = f32[128,96,96]{2,1,0:T(8,128)} copy(f32[128,96,96]{1,2,0:T(8,128)} %get-tuple-element.25) | data formatting | bytes 9437184
  96.7 6.5 %copy.33 = f32[128,96,96]{2,1,0:T(8,128)} copy(f32[128,96,96]{1,2,0:T(8,128)} %get-tuple-element.26) | data formatting | bytes 9437184 | tf_op jit(solution)/shard_map/slice | solution.py:43
  103.2 6.1 %pad_select_fusion = f32[128,97,96]{2,1,0:T(8,128)S(1)} fusion(f32[128,96,96]{2,1,0:T(8,128)} %get-tuple-element.27, f32[128,96,96]{2,1,0:T(8,128)} %copy.48, pred[97,96]{1,0:T(8,128)(4,1)S(1)} %iota_compare_fusion.6), kind=kLoop, calls=%fused_computation.3 | loop fusion | flops 1191936 | bytes 14214240 | tf_op jit(solution)/shard_map/jit(_where)/select_n | solution.py:49
  109.4 0.0 slice-done
  109.4 0.3 slice-done.1
  109.7 5.1 %pad_maximum_fusion = f32[128,193,96]{2,1,0:T(8,128)} fusion(f32[128,96,96]{2,1,0:T(8,128)S(1)} %bitcast.83, f32[128,97,96]{2,1,0:T(8,128)S(1)} %pad_select_fusion), kind=kLoop, calls=%fused_computation.1 | loop fusion | flops 2371584 | bytes 18972672 | tf_op jit(solution)/shard_map/concatenate | solution.py:50
  114.8 0.0 reduce-scatter.2.cloned.1.call-update
  114.8 127.0 %reduce-scatter.2.cloned.1.call-done = f32[8,193,96]{2,1,0:T(8,128)} async-done(((f32[128,193,96]{2,1,0:T(8,128)}), f32[8,193,96]{2,1,0:T(8,128)}) %reduce-scatter.2.cloned.1.call-update) | async-done | bytes 592912 | tf_op jit(solution)/shard_map/reduce_scatter | solution.py:104
  241.8 2.4 copy.34
  244.2 4.2 %all-to-all-start = ((f32[8,1,193,96]{2,3,1,0:T(8,128)}), f32[8,1,193,96]{2,3,1,0:T(8,128)S(1)}, u32[]{:S(2)}, u32[]{:S(2)}) async-start(f32[8,1,193,96]{2,3,1,0:T(8,128)} %copy.34), calls=%async_computation.1 | async-start | bytes 1572864 | tf_op jit(solution)/shard_map/all_to_all | solution.py:16
  248.4 0.0 copy-done.1
  248.4 0.7 dynamic_slice.3
  249.9 7.7 %all-to-all-done = f32[8,1,193,96]{2,3,1,0:T(8,128)S(1)} async-done(((f32[8,1,193,96]{2,3,1,0:T(8,128)}), f32[8,1,193,96]{2,3,1,0:T(8,128)S(1)}, u32[]{:S(2)}, u32[]{:S(2)}) %all-to-all-start) | async-done | bytes 592928 | tf_op jit(solution)/shard_map/all_to_all | solution.py:16
  257.5 0.1 reduce_sum.21
  257.6 0.1 fusion.10
  257.6 0.1 copy.40
  257.7 0.1 copy.49
  257.8 0.1 bitcast_select_fusion.1
  257.9 0.1 copy.39
  258.0 0.1 copy.41
  258.1 0.1 copy.42
  258.2 0.1 maximum_bitcast_fusion.1
  258.3 0.6 fusion.3
  259.6 0.1 maximum_add_fusion
  259.7 0.1 copy.43
  259.9 11.7 %custom-call.17 = f32[1,128,128]{2,1,0:T(8,128)S(1)} custom-call(f32[1,128,128]{2,1,0:T(8,128)S(1)} %cholesky.120), custom_call_target="Cholesky" | custom-call | tf_op jit(solution)/shard_map/jit(cholesky)/cholesky | solution.py:88
  271.7 9.8 %custom-call.18 = f32[1,1,128,128]{2,3,1,0:T(8,128)S(1)} custom-call(f32[1,1,128,128]{3,2,1,0:T(8,128)S(1)} %get-tuple-element.35), custom_call_target="InvertDiagBlocksLowerTriangular" | custom-call | tf_op jit(solution)/shard_map/jit(cholesky)/cholesky | solution.py:88
  281.5 0.2 bitcast_dynamic-update-slice_fusion
  281.7 0.2 fusion.2
  281.9 5.8 %custom-call.19 = f32[1,64,64]{2,1,0:T(8,128)S(1)} custom-call(f32[1,64,64]{2,1,0:T(8,128)S(1)} %fusion.2), custom_call_target="Cholesky" | custom-call | tf_op jit(solution)/shard_map/jit(cholesky)/cholesky | solution.py:88
  287.8 0.7 compare_reduce_fusion
  288.5 0.6 compare_reduce_fusion.1
  290.5 0.1 fusion.6
  290.6 19.7 %custom-call.20 = f32[1,2,128,128]{2,3,1,0:T(8,128)S(1)} custom-call(f32[1,2,128,128]{3,2,1,0:T(8,128)S(1)} %pad_maximum_fusion.1), custom_call_target="InvertDiagBlocksLowerTriangular" | custom-call | tf_op jit(solution)/shard_map/vmap(jit(_solve_triangular))/triangular_solve | solution.py:91
  310.3 0.3 fusion.5
  310.6 0.3 fusion.1
  310.9 0.3 convolution_bitcast_fusion
  311.3 0.1 copy.45
  311.4 0.1 broadcast_in_dim.35
  311.5 26.4 %all_to_all.10 = f32[8,1,192,192]{3,2,1,0:T(8,128)S(1)} all-to-all(f32[8,1,192,192]{3,2,1,0:T(8,128)S(1)} %broadcast_in_dim.35), channel_id=1, replica_groups=mesh['dp'=8,'head'=16] {'dp'}, dimensions={0} | all-to-all | bytes 2359296 | tf_op jit(solution)/shard_map/all_to_all | solution.py:22
  338.0 1.1 copy.54
  (19 shorter events, 0.2 us)
Async XLA Ops:
  6.5 235.3 %reduce-scatter.2.cloned.1.call-start = ((), (), s32[]{:S(2)}) async-start(), calls=%async_computation.3 | async-start | bytes 13926400 | tf_op jit(solution)/shard_map/reduce_scatter | solution.py:104
  6.6 24.6 %copy-start = (s32[384]{0:T(512)S(1)}, s32[384]{0:T(512)}, u32[]{:S(2)}) copy-start(s32[384]{0:T(512)} %param.4) | copy-start | bytes 4612
  103.2 6.1 %slice-start = ((s8[6291456]{0:T(1024)(128)(4,1)}), s8[4194304]{0:T(1024)(128)(4,1)S(1)}, s32[]{:S(2)}) async-start(s8[6291456]{0:T(1024)(128)(4,1)} %bitcast.82), calls=%async_computation.4 | async-start | bytes 8388608
  103.2 6.5 %slice-start.1 = ((s8[6291456]{0:T(1024)(128)(4,1)}), s8[2097152]{0:T(1024)(128)(4,1)S(1)}, s32[]{:S(2)}) async-start(s8[6291456]{0:T(1024)(128)(4,1)} %bitcast.82), calls=%async_computation.5 | async-start | bytes 4194304
  114.8 133.6 %copy-start.1 = (s32[128]{0:T(128)S(1)}, s32[128]{0:T(128)}, u32[]{:S(2)}) copy-start(s32[128]{0:T(128)} %param.5) | copy-start | bytes 1540
  244.2 13.3 %all-to-all-start = ((f32[8,1,193,96]{2,3,1,0:T(8,128)}), f32[8,1,193,96]{2,3,1,0:T(8,128)S(1)}, u32[]{:S(2)}, u32[]{:S(2)}) async-start(f32[8,1,193,96]{2,3,1,0:T(8,128)} %copy.34), calls=%async_computation.1 | async-start | bytes 1572864 | tf_op jit(solution)/shard_map/all_to_all | solution.py:16
Sparse Core Ops, SparseCore 0:
  114.9 126.8 reduce-scatter.1
where the time goes:
time: 348 us; the launch traced here: 346 us
  waiting for transfers between devices  135 us (39%)
  other arithmetic  77.5 us (22%)
  local copies, waits for them, and re-layouts  61.8 us (18%)
  blocking collectives  26.4 us (8%)
  matrix products  25 us (7%)
  between operations  16.4 us (5%)
  starting transfers between devices  4.19 us (1%)
    reduce_scatter x1, waiting for transfers between devices, on_device(): lax.psum_scatter(encode(block_grams(projected, scaled, lax.axis_size('hea...  127 us
    unnamed x12, local copies, waits for them, and re-layouts  32.8 us
    another operation x7, other arithmetic, whiten(): lower = jnp.linalg.cholesky(damped)  28.8 us
    all_to_all x1, blocking collectives, from_everyone(): lax.all_to_all(jnp.broadcast_to(shard[None], (length, *shard.shape)), axi...  26.4 us
    dot_general x1, matrix products, block_grams(): jnp.einsum('tch,tcg->chg', left, right, preferred_element_type=jnp.float32)  23.7 us
    another operation x6, other arithmetic, invert(): return jax.scipy.linalg.solve_triangular(factor, eye, lower=True)  19.8 us
    slice x1, local copies, waits for them, and re-layouts, pack_sym(): upper_left = full[..., :half, :half]  18.7 us
    mul x1, other arithmetic, on_device(): scaled = projected * weights[:, None]  16.5 us
  transfers between devices with their start and end apart: 2, of which 2 were waited for; matrix products, arithmetic and copies ran while one was open for 0% of the time, Pallas kernels for 0%

commit v1 on v0

v1 whole, which is shorter than its diff:
```python
import functools
import jax
import jax.numpy as jnp
from jax import lax
from jax.experimental import pallas as pl
from jax.experimental.pallas import tpu as pltpu
from jax.sharding import PartitionSpec as P

HD = 192
ROWS = 56
MESH = pl.DeviceIdType.MESH
F32 = jnp.float32


def tdot(a, b):
    return lax.dot_general(a, b, (((0,), (0,)), ((), ())), preferred_element_type=F32)


def place():
    dp, head = lax.axis_index("dp"), lax.axis_index("head")
    x, y, z = head // 4, (head // 2) % 2 * 2 + dp // 4, dp % 4
    return x, y, z, head % 2


def device(x, y, z, core):
    return (y % 2 * 4 + z, x * 4 + y // 2 * 2 + core)


def rel(step):
    return (2 - step + (step // 2) * (7 - 2 * step)) % 4


def pack(low, high, put):
    r = lax.broadcasted_iota(jnp.int32, (128, 128), 0)
    c = lax.broadcasted_iota(jnp.int32, (128, 128), 1)
    odd = high[:, 128:]
    left = c < 64
    a = jnp.where(r >= c, low[:128, :128], odd)
    b = jnp.where(left, low[:128, 128:], high[:, :128])
    e = jnp.where(left[:64], low[128:192, 128:], low[192:, 128:])
    d = jnp.sum(jnp.where(r == c, odd, 0.0), axis=0, keepdims=True)
    put(0, 0, 0, a[:56])
    put(0, 1, 0, a[56:112])
    put(0, 2, 0, a[112:])
    put(0, 2, 16, b[:40])
    put(1, 0, 0, b[40:96])
    put(1, 1, 0, b[96:])
    put(1, 1, 32, e[:24])
    put(1, 2, 0, e[24:])
    put(1, 2, 40, jnp.broadcast_to(d, (16, 128)))


def dot(a, b, ca, cb):
    return lax.dot_general(a, b, (((ca,), (cb,)), ((), ())), precision=lax.Precision.HIGHEST,
                           preferred_element_type=F32)


def mul(a, b):
    return dot(a, b, 1, 0)


def mul_t(a, b):
    return dot(a, b, 1, 1)


def inverse_factor(d):
    r = lax.broadcasted_iota(jnp.int32, (64, 64), 0)
    c = lax.broadcasted_iota(jnp.int32, (64, 64), 1)
    full = jnp.concatenate([d, (r == c).astype(F32)], axis=1)
    m = [full[8 * i:8 * i + 8] for i in range(8)]
    sub = lax.broadcasted_iota(jnp.int32, (8, 128), 0)
    out = []

    def row(v, j):
        return jnp.broadcast_to(v[j:j + 1], (8, 128))

    for k in range(8):
        cs = {(i, j): jnp.broadcast_to(m[i][:, 8 * k + j:8 * k + j + 1], (8, 128))
              for i in range(k, 8) for j in range(8)}
        diag = jnp.ones((8, 128), F32)
        for j in range(8):
            pivot = row(cs[k, j], j)
            diag = jnp.where(sub == j, pivot, diag)
            inv = 1.0 / pivot
            scaled = row(m[k], j) * inv
            below = jnp.where(sub > j, cs[k, j], 0.0)
            us = {n: row(cs[k, n], j) * inv for n in range(j + 1, 8)}
            for i in range(k, 8):
                f = below if i == k else cs[i, j]
                m[i] = m[i] - f * scaled
                for n in range(j + 1, 8):
                    cs[i, n] = cs[i, n] - f * us[n]
        out.append((m[k] * lax.rsqrt(diag))[:, 64:])
    return jnp.concatenate(out, axis=0)


def whiten(flat, even, scale, total):
    r = lax.broadcasted_iota(jnp.int32, (128, 128), 0)
    c = lax.broadcasted_iota(jnp.int32, (128, 128), 1)
    flat = flat / total
    a, bc = flat[:128], flat[128:320]
    t = a.T
    low = jnp.where(r >= c, a, t)
    high = jnp.where(r < c, a, jnp.where(r == c, flat[320:321], t))
    a = jnp.where(even, low, high)
    b = jnp.where(even, bc[:, :64], bc[:, 64:])
    b0, b1, corner = b[:64], b[64:128], b[128:]
    a00, a10, a11 = a[:64, :64], a[64:, :64], a[64:, 64:]
    g00 = jnp.where(even, a00, corner)
    g10 = jnp.where(even, a10, b0)
    g11 = jnp.where(even, a11, a00)
    g20 = jnp.where(even, b0.T, b1)
    g21 = jnp.where(even, b1.T, a10)
    g22 = jnp.where(even, corner, a11)
    eye = r[:64, :64] == c[:64, :64]
    diag = jnp.where(eye, g00 + g11 + g22, 0.0)
    level = jnp.sum(jnp.sum(diag, axis=0, keepdims=True), axis=1, keepdims=True) / HD + 1e-06
    damp = jnp.where(eye, scale * level, 0.0)

    w00 = inverse_factor(g00 + damp)
    l10, l20 = mul_t(g10, w00), mul_t(g20, w00)
    s11 = g11 + damp - mul_t(l10, l10)
    s21 = g21 - mul_t(l20, l10)
    s22 = g22 + damp - mul_t(l20, l20)
    x10, x20 = mul(l10, w00), mul(l20, w00)
    w11 = inverse_factor(s11)
    l21 = mul_t(s21, w11)
    s22 = s22 - mul_t(l21, l21)
    w10 = -mul(w11, x10)
    x21 = mul(l21, w11)
    x20 = x20 + mul(l21, w10)
    w22 = inverse_factor(s22)
    return w00, w10, w11, -mul(w22, x20), -mul(w22, x21), w22


def whitening_kernel(total, x_ref, w_ref, damp_ref, out_ref, own, got, asem, bsem, xb, g, pr, rl, rr, fl, fr, f1, q2l, q2r, f2l, f2r, f2, f3, h,
                  xsem, dsend, drecv, rsem, ssem, fsem, s2send, q2sem, f2sem, s3send, s3sem, hsem):
    x, y, z, core = place()
    partner = device(x, y, z, 1 - core)
    right = (device((x + 1) % 4, y, z, core), device(x, (y + 1) % 4, z, core), device(x, y, (z + 1) % 4, core))
    left = (device((x + 3) % 4, y, z, core), device(x, (y + 3) % 4, z, core), device(x, y, (z + 3) % 4, core))
    far = (device((x + 2) % 4, y, z, core), device(x, (y + 2) % 4, z, core), device(x, y, (z + 2) % 4, core))

    def fetch(s, i):
        px = (x + rel(s // 2)) % 4
        py = (y + rel(s % 2 * 2 + i // 4)) % 4
        pz = (z + rel(i % 4)) % 4
        col = pl.multiple_of((px * 16 + py * 4 + pz) * 384, 384)
        return pltpu.make_async_copy(x_ref.at[:, pl.ds(col, 384)], xb.at[s % 2, i], xsem.at[s % 2, i])

    for i in range(8):
        fetch(0, i).start()

    barrier = pltpu.get_barrier_semaphore()
    base_y, low_y = y // 2 * 2, y % 2
    peers = [device(x, base_y + dy, (z + dz) % 4, cc) for dy in range(2) for dz in range(1, 4) for cc in range(2)]
    peers += [partner, device(x, base_y + 1 - low_y, z, 0), device(x, base_y + 1 - low_y, z, 1)]
    peers += [device((x + k) % 4, y, z, core) for k in range(1, 4)]
    peers += [device(x, (base_y + 2) % 4 + dy, z, core) for dy in range(2)]
    for peer in peers:
        pl.semaphore_signal(barrier, inc=1, device_id=peer, device_id_type=MESH)
    pl.semaphore_wait(barrier, len(peers))

    def remote(src, dst, send, recv, to):
        return pltpu.make_async_remote_copy(src_ref=src, dst_ref=dst, send_sem=send, recv_sem=recv,
                                            device_id=to, device_id_type=MESH)

    def halves(s):
        at = pl.ds(s * 8, 8)
        return remote(g.at[1 - core, :, at], pr.at[:, at], dsend, drecv.at[s], partner)

    def mine(col, first, count):
        return g.at[core, col, pl.ds(first, count)]

    def to_right(col, src, dst, sem):
        remote(src, dst, ssem.at[col, 0], sem, right[col]).start()

    def to_left(col, src, dst, sem):
        remote(src, dst, ssem.at[col, 1], sem, left[col]).start()

    def final_right(col, first, count, at):
        to_right(col, mine(col, first, count), fl.at[col, pl.ds(at, count)], fsem.at[col, 0])

    def final_left(col, first, count, at):
        to_left(col, mine(col, first, count), fr.at[col, pl.ds(at, count)], fsem.at[col, 1])

    def relay_right(col, first, count, at, sem):
        to_right(col, mine(col, first, count), rl.at[col, pl.ds(at, count)], rsem.at[0, sem])

    def relay_left(col, first, count, at, sem):
        to_left(col, mine(col, first, count), rr.at[col, pl.ds(at, count)], rsem.at[1, sem])

    def taken(buf, side, col, first, count, at, sem):
        part = buf.at[col, pl.ds(at, count)]
        remote(part, part, ssem.at[col, 0], rsem.at[side, sem], right[col]).wait_recv()
        g[core, col, pl.ds(first, count)] += buf[col, pl.ds(at, count)]

    def grams(s):
        for i in range(8):
            fetch(s, i).wait()

        w = w_ref[...]
        w3 = jnp.concatenate([w, w, w], axis=1)
        for i in range(8):
            t = xb[s % 2, i]
            tw = t * w3
            low = tdot(t[:, :256], tw[:, :256])
            high = tdot(t[:, 256:], tw[:, 128:])

            def put(half, col, row, value):
                g[half, col, s * 8 + i, pl.ds(row, value.shape[0]), :] = value

            pack(low, high, put)
        halves(s).start()

    def summed(s):
        base = s * 8
        halves(s).wait_recv()
        for col in range(3):
            g[core, col, pl.ds(base, 8)] += pr[col, pl.ds(base, 8)]
        xs, yh = s // 2, s % 2

        @pl.when(xs == 0)
        def _():
            relay_right(0, base, 4, yh * 4, yh)
            relay_left(0, base + 4, 4, yh * 4, yh)

        @pl.when(xs == 1)
        def _():
            final_right(0, base + 4, 4, yh * 8 + 4)

        @pl.when(xs == 2)
        def _():
            final_left(0, base, 4, yh * 8)

        @pl.when(yh == 0)
        def _():
            relay_right(1, base, 2, xs * 2, 2 + xs)
            relay_left(1, base + 2, 2, xs * 2, 2 + xs)
            final_right(1, base + 6, 2, xs * 4 + 2)

        @pl.when(yh == 1)
        def _():
            final_left(1, base, 2, xs * 4)

        relay_right(2, base, 1, s, 6 + s)
        relay_left(2, base + 4, 1, s, 6 + s)
        final_right(2, base + 5, 1, s * 2 + 1)
        final_left(2, base + 2, 1, s * 2)

    def passed(s):
        base = s * 8
        xs, yh = s // 2, s % 2

        @pl.when(xs == 1)
        def _():
            taken(rl, 0, 0, base, 4, yh * 4, yh)
            final_right(0, base, 4, yh * 8)

        @pl.when(xs == 2)
        def _():
            taken(rr, 1, 0, base + 4, 4, yh * 4, yh)
            final_left(0, base + 4, 4, yh * 8 + 4)

        @pl.when(yh == 0)
        def _():
            taken(rl, 0, 1, base + 4, 2, xs * 2, 2 + xs)
            final_right(1, base + 4, 2, xs * 4)

        @pl.when(yh == 1)
        def _():
            taken(rr, 1, 1, base + 2, 2, xs * 2, 2 + xs)
            final_left(1, base + 2, 2, xs * 4 + 2)

        taken(rl, 0, 2, base + 1, 1, s, 6 + s)
        final_right(2, base + 1, 1, s * 2)
        taken(rr, 1, 2, base + 6, 1, s, 6 + s)
        final_left(2, base + 6, 1, s * 2 + 1)

    def step(s, carry):
        @pl.when(s < 7)
        def _():
            for i in range(8):
                fetch(s + 1, i).start()

        grams(s)

        @pl.when(s >= 1)
        def _():
            summed(s - 1)

        @pl.when(s >= 2)
        def _():
            passed(s - 2)

        return carry

    lax.fori_loop(0, 8, step, 0)
    summed(7)
    passed(6)
    passed(7)

    axis2, axis3 = (1, 2, 0), (2, 0, 1)
    for col in range(3):
        for buf, side, to in ((fl, 0, left), (fr, 1, right)):
            remote(buf.at[col], buf.at[col], ssem.at[col, side], fsem.at[col, side], to[col]).wait_recv()
        for a in range(4):
            for b in range(4):
                slot = (48 + a * 4 + b, (2 * a + 1) * 8 + 4 + b, (2 * a + b // 2) * 8 + 3 + 4 * (b % 2))[col]
                at = b * 4 + a if col == 1 else a * 4 + b
                f1[col, at] = g[core, col, slot] + fl[col, a * 4 + b] + fr[col, a * 4 + b]
        ax = axis2[col]

        def part(first):
            return f1.at[col, pl.ds(first, 2)]

        remote(part(0), q2l.at[col], s2send.at[col, 0], q2sem.at[col, 0], right[ax]).start()
        remote(part(2), q2r.at[col], s2send.at[col, 1], q2sem.at[col, 1], left[ax]).start()
        remote(part(6), f2l.at[col, pl.ds(2, 2)], s2send.at[col, 0], f2sem.at[col, 0], right[ax]).start()
        remote(part(8), f2r.at[col, pl.ds(0, 2)], s2send.at[col, 1], f2sem.at[col, 1], left[ax]).start()
    for col in range(3):
        ax = axis2[col]
        remote(q2l.at[col], q2l.at[col], s2send.at[col, 0], q2sem.at[col, 0], right[ax]).wait_recv()
        f1[col, pl.ds(4, 2)] += q2l[col]
        remote(f1.at[col, pl.ds(4, 2)], f2l.at[col, pl.ds(0, 2)], s2send.at[col, 0], f2sem.at[col, 0], right[ax]).start()
        remote(q2r.at[col], q2r.at[col], s2send.at[col, 1], q2sem.at[col, 1], left[ax]).wait_recv()
        f1[col, pl.ds(10, 2)] += q2r[col]
        remote(f1.at[col, pl.ds(10, 2)], f2r.at[col, pl.ds(2, 2)], s2send.at[col, 1], f2sem.at[col, 1], left[ax]).start()
    for col in range(3):
        ax, ax3 = axis2[col], axis3[col]
        remote(f2l.at[col], f2l.at[col], s2send.at[col, 0], f2sem.at[col, 0], right[ax]).wait_recv()
        remote(f2r.at[col], f2r.at[col], s2send.at[col, 1], f2sem.at[col, 1], left[ax]).wait_recv()
        f2[col] = f1[col, pl.ds(12, 4)] + f2l[col] + f2r[col]
        for k, to in enumerate((far, right, left)):
            remote(f2.at[col, k], f3.at[col, k], s3send.at[col, k], s3sem.at[col, k], to[ax3]).start()
    for col in range(3):
        for k, to in enumerate((far, right, left)):
            remote(f2.at[col, k], f3.at[col, k], s3send.at[col, k], s3sem.at[col, k], to[axis3[col]]).wait_recv()
        h[core, col] = (f2[col, 3] + f3[col, 0]) + (f3[col, 1] + f3[col, 2])
    both = remote(h.at[core], h.at[core], hsem.at[0], hsem.at[1], partner)
    both.start()
    both.wait_recv()
    flat = jnp.concatenate([h[half, col] for half in range(2) for col in range(3)], axis=0)
    owner = (x * 16 + y * 4 + z) * 2 + core
    w00, w10, w11, w20, w21, w22 = whiten(flat, core == 0, damp_ref[owner], total)
    slot = z * 2 + core
    own[0:64] = jnp.concatenate([w00, w22], axis=1)
    own[64:128] = jnp.concatenate([w10, w11], axis=1)
    own[128:192] = jnp.concatenate([w20, w21], axis=1)

    def spread(k):
        to = device(x, base_y + (low_y + 1 - k // 4) % 2, (z + (2, 1, 3, 0)[k % 4]) % 4, low_y)
        return remote(own, got.at[slot], asem, bsem.at[slot], to)

    for k in range(7):
        spread(k).start()

    @pl.when(core != low_y)
    def _():
        spread(7).start()

    @pl.when(core == low_y)
    def _():
        got[slot] = own[...]

    for j in range(8):
        @pl.when(jnp.logical_or(core != low_y, slot != j))
        def _():
            remote(got.at[j], got.at[j], asem, bsem.at[j], partner).wait_recv()

        out_ref[j, 0:64, 0:64] = got[j, 0:64, 0:64]
        out_ref[j, 0:64, 64:192] = jnp.zeros((64, 128), F32)
        out_ref[j, 64:128, 0:128] = got[j, 64:128]
        out_ref[j, 64:128, 128:192] = jnp.zeros((64, 64), F32)
        out_ref[j, 128:192, 0:128] = got[j, 128:192]
        out_ref[j, 128:192, 128:192] = got[j, 0:64, 64:128]

    for col in range(3):
        for side in range(2):
            sent = g.at[core, col, pl.ds(0, 24)]
            remote(sent, sent, ssem.at[col, side], fsem.at[col, side], right[col]).wait_send()
            six = f1.at[col, pl.ds(0, 6)]
            remote(six, six, s2send.at[col, side], f2sem.at[col, side], right[col]).wait_send()
        for k in range(3):
            remote(f2.at[col, k], f3.at[col, k], s3send.at[col, k], s3sem.at[col, k], right[col]).wait_send()
    every = g.at[1 - core]
    remote(every, pr, dsend, drecv.at[0], partner).wait_send()
    both.wait_send()
    seven = got.at[pl.ds(0, 7)]
    remote(seven, seven, asem, bsem.at[0], partner).wait_send()

    @pl.when(core != low_y)
    def _():
        remote(got.at[0], got.at[0], asem, bsem.at[0], partner).wait_send()


def on_device(projected, weight_exp, damp_exp):
    weights = jnp.exp2(weight_exp.astype(F32)).astype(jnp.bfloat16)
    wide = jnp.broadcast_to(weights[:, None], (weights.shape[0], 128))
    scale = jnp.exp2(-damp_exp.astype(F32))
    total = projected.shape[0] * lax.axis_size('dp') * lax.axis_size('head')
    unit = (ROWS, 128)
    dma = pltpu.SemaphoreType.DMA
    return pl.pallas_call(
        functools.partial(whitening_kernel, total),
        out_shape=jax.ShapeDtypeStruct((8, HD, HD), F32),
        in_specs=[pl.BlockSpec(memory_space=pl.ANY), pl.BlockSpec(memory_space=pltpu.VMEM),
                  pl.BlockSpec(memory_space=pltpu.SMEM)],
        out_specs=pl.BlockSpec(memory_space=pltpu.VMEM),
        scratch_shapes=[
            pltpu.VMEM((HD, 128), F32), pltpu.VMEM((8, HD, 128), F32), dma, dma((8,)),
            pltpu.VMEM((2, 8, 384, 384), jnp.bfloat16),
            pltpu.VMEM((2, 3, 64) + unit, F32),
            pltpu.VMEM((3, 64) + unit, F32),
            pltpu.VMEM((3, 8) + unit, F32),
            pltpu.VMEM((3, 8) + unit, F32),
            pltpu.VMEM((3, 16) + unit, F32),
            pltpu.VMEM((3, 16) + unit, F32),
            pltpu.VMEM((3, 16) + unit, F32),
            pltpu.VMEM((3, 2) + unit, F32),
            pltpu.VMEM((3, 2) + unit, F32),
            pltpu.VMEM((3, 4) + unit, F32),
            pltpu.VMEM((3, 4) + unit, F32),
            pltpu.VMEM((3, 4) + unit, F32),
            pltpu.VMEM((3, 3) + unit, F32),
            pltpu.VMEM((2, 3) + unit, F32),
            dma((2, 8)), dma, dma((8,)), dma((2, 14)), dma((3, 2)), dma((3, 2)),
            dma((3, 2)), dma((3, 2)), dma((3, 2)), dma((3, 3)), dma((3, 3)), dma((2,)),
        ],
        compiler_params=pltpu.CompilerParams(collective_id=0, has_side_effects=True, vmem_limit_bytes=58 * 2**20),
        name="whitening",
    )(projected, wide, scale)


def solution(mesh):
    return jax.shard_map(
        on_device,
        mesh=mesh,
        in_specs=(P(("dp", "head"), None), P(("dp", "head")), P()),
        out_specs=P("head", None, None),
        check_vma=False,
    )
```

time: 348 us -> 72.8 us (0.21)
  waiting for transfers between devices: 135 us -> 0 us
  other arithmetic: 77.5 us -> 1.89 us
  Pallas kernels: 0 us -> 67.2 us
  local copies, waits for them, and re-layouts: 61.8 us -> 3.42 us
  blocking collectives: 26.4 us -> 0 us
  matrix products: 25 us -> 0 us
  between operations: 16.4 us -> 0.01 us
  starting transfers between devices: 4.19 us -> 0 us
    reduce_scatter x1 -> x0, waiting for transfers between devices: 127 us -> none  [on_device(): lax.psum_scatter(encode(block_grams(projected, scaled, lax.axis_size('hea...]
    pallas_call x0 -> x1, Pallas kernels: none -> 67.2 us  [on_device(): pl.pallas_call(functools.partial(whitening_kernel, total), out_shape=jax....]
    another operation x13 -> x0, other arithmetic: 48.6 us -> none  [the longest x7 28.8 us: whiten(): lower = jnp.linalg.cholesky(damped)]
    unnamed x12 -> x1, local copies, waits for them, and re-layouts: 32.8 us -> 2.65 us
    all_to_all x1 -> x0, blocking collectives: 26.4 us -> none  [from_everyone(): lax.all_to_all(jnp.broadcast_to(shard[None], (length, *shard.shape)), axi...]
    slice x5 -> x0, local copies, waits for them, and re-layouts: 25.5 us -> none  [the longest x1 18.7 us: pack_sym(): upper_left = full[..., :half, :half]]
    dot_general x1 -> x0, matrix products: 23.7 us -> none  [block_grams(): jnp.einsum('tch,tcg->chg', left, right, preferred_element_type=jnp.float32)]
    mul x1 -> x0, other arithmetic: 16.5 us -> none  [on_device(): scaled = projected * weights[:, None]]
  transfers between devices with their start and end apart: 2 -> 0, of which waited for: 2 -> 0; matrix products, arithmetic and copies ran while one was open for 0% -> 0% of each run, Pallas kernels for 0% -> 0%
where the time goes in v1:
time: 72.8 us; the launch traced here: 72.5 us
  Pallas kernels  67.2 us (92%)
  local copies, waits for them, and re-layouts  3.42 us (5%)
  other arithmetic  1.89 us (3%)
    pallas_call x1, Pallas kernels, on_device(): pl.pallas_call(functools.partial(whitening_kernel, total), out_shape=jax....  67.2 us
    unnamed x1, local copies, waits for them, and re-layouts  2.65 us

profile of v1, /device:TPU:1, one launch (start us, length us, event | category | flops | bytes accessed | tf_op | source)
XLA Modules:
  0.0 72.5 jit_solution(16691613728182986582)
XLA Ops:
  0.0 1.2 %multiply_exponential_fusion.damp_ref = f32[128]{0:T(128)} fusion(s32[128]{0:T(128)} %param.5), kind=kLoop, calls=%fused_computation.1 | loop fusion | flops 384 | bytes 1024 | tf_op jit(solution)/shard_map/exp2 | solution.py:400
  1.2 0.7 exponential_convert_fusion
  1.9 0.8 %broadcast_in_dim.2.w_ref = bf16[384,128]{1,0:T(8,128)(2,1)} broadcast(bf16[384]{0:T(512)(128)(2,1)S(1)} %exponential_convert_fusion), dimensions={0} | broadcast | bytes 99072 | tf_op jit(solution)/shard_map/broadcast_in_dim | solution.py:399
  2.7 67.2 %whitening.1 = f32[8,192,192]{2,1,0:T(8,128)} custom-call(bf16[384,24576]{1,0:T(8,128)(2,1)} %x_ref.1, bf16[384,128]{1,0:T(8,128)(2,1)} %broadcast_in_dim.2.w_ref, f32[128]{0:T(128)} %multiply_exponential_fusion.damp_ref), custom_call_target="tpu_custom_call" | custom-call | tf_op jit(solution)/shard_map/whitening/pallas_call | solution.py:404
  69.8 2.7 %copy.5 = f32[8,192,192]{2,1,0:T(8,128)} copy(f32[8,192,192]{2,1,0:T(8,128)} %whitening.1) | data formatting | bytes 2359296

commit v2 on v1

--- a/solution.py
+++ b/solution.py
@@ -8,6 +8,8 @@
 
 HD = 192
 ROWS = 56
+OUT = pltpu.VMEM
+LAG = 8
 MESH = pl.DeviceIdType.MESH
 F32 = jnp.float32
 
@@ -94,7 +96,11 @@
     return jnp.concatenate(out, axis=0)
 
 
-def whiten(flat, even, scale, total):
+def folded(a):
+    return jnp.concatenate([a[:32], a[32:]], axis=1)
+
+
+def whiten(flat, even, scale, total, emit):
     r = lax.broadcasted_iota(jnp.int32, (128, 128), 0)
     c = lax.broadcasted_iota(jnp.int32, (128, 128), 1)
     flat = flat / total
@@ -118,6 +124,7 @@
     damp = jnp.where(eye, scale * level, 0.0)
 
     w00 = inverse_factor(g00 + damp)
+    emit(0, 32, folded(w00))
     l10, l20 = mul_t(g10, w00), mul_t(g20, w00)
     s11 = g11 + damp - mul_t(l10, l10)
     s21 = g21 - mul_t(l20, l10)
@@ -127,13 +134,15 @@
     l21 = mul_t(s21, w11)
     s22 = s22 - mul_t(l21, l21)
     w10 = -mul(w11, x10)
+    emit(32, 64, jnp.concatenate([w10, w11], axis=1))
     x21 = mul(l21, w11)
     x20 = x20 + mul(l21, w10)
     w22 = inverse_factor(s22)
-    return w00, w10, w11, -mul(w22, x20), -mul(w22, x21), w22
-
-
-def whitening_kernel(total, x_ref, w_ref, damp_ref, out_ref, own, got, asem, bsem, xb, g, pr, rl, rr, fl, fr, f1, q2l, q2r, f2l, f2r, f2, f3, h,
+    last = jnp.concatenate([-mul(w22, x20), -mul(w22, x21)], axis=1)
+    emit(96, 96, jnp.concatenate([last, folded(w22)], axis=0))
+
+
+def whitening_kernel(total, x_ref, weight_ref, damp_ref, got, wexp, dexp, w_ref, esem, own, asem, bsem, xb, g, pr, rl, rr, fl, fr, f1, q2l, q2r, f2l, f2r, f2, f3, h,
                   xsem, dsend, drecv, rsem, ssem, fsem, s2send, q2sem, f2sem, s3send, s3sem, hsem):
     x, y, z, core = place()
     partner = device(x, y, z, 1 - core)
@@ -150,6 +159,10 @@
 
     for i in range(8):
         fetch(0, i).start()
+
+    exps = (pltpu.make_async_copy(weight_ref, wexp, esem.at[0]), pltpu.make_async_copy(damp_ref, dexp, esem.at[1]))
+    for copy in exps:
+        copy.start()
 
     barrier = pltpu.get_barrier_semaphore()
     base_y, low_y = y // 2 * 2, y % 2
@@ -159,7 +172,11 @@
     peers += [device(x, (base_y + 2) % 4 + dy, z, core) for dy in range(2)]
     for peer in peers:
         pl.semaphore_signal(barrier, inc=1, device_id=peer, device_id_type=MESH)
-    pl.semaphore_wait(barrier, len(peers))
+    for copy in exps:
+        copy.wait()
+    for k in range(3):
+        line = jnp.exp2(wexp[pl.ds(128 * k, 128)].astype(F32)).reshape(1, 128)
+        w_ref[pl.ds(128 * k, 128)] = jnp.broadcast_to(line, (128, 128)).T.astype(jnp.bfloat16)
 
     def remote(src, dst, send, recv, to):
         return pltpu.make_async_remote_copy(src_ref=src, dst_ref=dst, send_sem=send, recv_sem=recv,
@@ -211,6 +228,11 @@
                 g[half, col, s * 8 + i, pl.ds(row, value.shape[0]), :] = value
 
             pack(low, high, put)
+
+        @pl.when(s == 0)
+        def _():
+            pl.semaphore_wait(barrier, len(peers))
+
         halves(s).start()
 
     def summed(s):
@@ -289,16 +311,20 @@
         def _():
             summed(s - 1)
 
-        @pl.when(s >= 2)
-        def _():
-            passed(s - 2)
+        @pl.when(s >= LAG)
+        def _():
+            passed(s - LAG)
 
         return carry
 
     lax.fori_loop(0, 8, step, 0)
     summed(7)
-    passed(6)
-    passed(7)
+
+    def rest(s, carry):
+        passed(s)
+        return carry
+
+    lax.fori_loop(8 - LAG, 8, rest, 0)
 
     axis2, axis3 = (1, 2, 0), (2, 0, 1)
     for col in range(3):
@@ -342,38 +368,32 @@
     both.wait_recv()
     flat = jnp.concatenate([h[half, col] for half in range(2) for col in range(3)], axis=0)
     owner = (x * 16 + y * 4 + z) * 2 + core
-    w00, w10, w11, w20, w21, w22 = whiten(flat, core == 0, damp_ref[owner], total)
+    lane = lax.broadcasted_iota(jnp.int32, (1, 128), 1)
+    exponent = jnp.where(lane == owner, dexp[...].astype(F32).reshape(1, 128), 0.0)
+    scale = jnp.exp2(-jnp.sum(exponent, axis=1, keepdims=True))
     slot = z * 2 + core
-    own[0:64] = jnp.concatenate([w00, w22], axis=1)
-    own[64:128] = jnp.concatenate([w10, w11], axis=1)
-    own[128:192] = jnp.concatenate([w20, w21], axis=1)
-
-    def spread(k):
-        to = device(x, base_y + (low_y + 1 - k // 4) % 2, (z + (2, 1, 3, 0)[k % 4]) % 4, low_y)
-        return remote(own, got.at[slot], asem, bsem.at[slot], to)
-
-    for k in range(7):
-        spread(k).start()
-
-    @pl.when(core != low_y)
-    def _():
-        spread(7).start()
-
-    @pl.when(core == low_y)
-    def _():
-        got[slot] = own[...]
+
+    def emit(first, count, value):
+        rows = pl.ds(first, count)
+        own[rows] = value
+        for k in range(8):
+            to = device(x, base_y + (low_y + 1 - k // 4) % 2, (z + (2, 1, 3, 0)[k % 4]) % 4, low_y)
+            copy = remote(own.at[rows], got.at[slot, rows], asem, bsem.at[slot], to)
+            if k < 7:
+                copy.start()
+            else:
+                pl.when(core != low_y)(copy.start)
+
+        @pl.when(core == low_y)
+        def _():
+            got[slot, rows] = value
+
+    whiten(flat, core == 0, scale, total, emit)
 
     for j in range(8):
         @pl.when(jnp.logical_or(core != low_y, slot != j))
         def _():
             remote(got.at[j], got.at[j], asem, bsem.at[j], partner).wait_recv()
-
-        out_ref[j, 0:64, 0:64] = got[j, 0:64, 0:64]
-        out_ref[j, 0:64, 64:192] = jnp.zeros((64, 128), F32)
-        out_ref[j, 64:128, 0:128] = got[j, 64:128]
-        out_ref[j, 64:128, 128:192] = jnp.zeros((64, 64), F32)
-        out_ref[j, 128:192, 0:128] = got[j, 128:192]
-        out_ref[j, 128:192, 128:192] = got[j, 0:64, 64:128]
 
     for col in range(3):
         for side in range(2):
@@ -394,21 +414,36 @@
         remote(got.at[0], got.at[0], asem, bsem.at[0], partner).wait_send()
 
 
+def unpack_kernel(packed, out_ref, full, sem):
+    copies = []
+    for j in range(8):
+        full[j, 0:32, 0:64] = packed[j, 0:32, 0:64]
+        full[j, 32:64, 0:64] = packed[j, 0:32, 64:128]
+        full[j, 0:64, 64:192] = jnp.zeros((64, 128), F32)
+        full[j, 64:128, 0:128] = packed[j, 32:96]
+        full[j, 64:128, 128:192] = jnp.zeros((64, 64), F32)
+        full[j, 128:192, 0:128] = packed[j, 96:160]
+        full[j, 128:160, 128:192] = packed[j, 160:192, 0:64]
+        full[j, 160:192, 128:192] = packed[j, 160:192, 64:128]
+        copies.append(pltpu.make_async_copy(full.at[j], out_ref.at[j], sem.at[j]))
+        copies[-1].start()
+    for copy in copies:
+        copy.wait()
+
+
 def on_device(projected, weight_exp, damp_exp):
-    weights = jnp.exp2(weight_exp.astype(F32)).astype(jnp.bfloat16)
-    wide = jnp.broadcast_to(weights[:, None], (weights.shape[0], 128))
-    scale = jnp.exp2(-damp_exp.astype(F32))
     total = projected.shape[0] * lax.axis_size('dp') * lax.axis_size('head')
     unit = (ROWS, 128)
     dma = pltpu.SemaphoreType.DMA
-    return pl.pallas_call(
+    packed = pl.pallas_call(
         functools.partial(whitening_kernel, total),
-        out_shape=jax.ShapeDtypeStruct((8, HD, HD), F32),
-        in_specs=[pl.BlockSpec(memory_space=pl.ANY), pl.BlockSpec(memory_space=pltpu.VMEM),
-                  pl.BlockSpec(memory_space=pltpu.SMEM)],
+        out_shape=OUT((8, HD, 128), F32),
+        in_specs=[pl.BlockSpec(memory_space=pl.ANY), pl.BlockSpec(memory_space=pl.ANY),
+                  pl.BlockSpec(memory_space=pl.ANY)],
         out_specs=pl.BlockSpec(memory_space=pltpu.VMEM),
         scratch_shapes=[
-            pltpu.VMEM((HD, 128), F32), pltpu.VMEM((8, HD, 128), F32), dma, dma((8,)),
+            pltpu.VMEM((384,), jnp.int32), pltpu.VMEM((128,), jnp.int32), pltpu.VMEM((384, 128), jnp.bfloat16), dma((2,)),
+            pltpu.VMEM((HD, 128), F32), dma, dma((8,)),
             pltpu.VMEM((2, 8, 384, 384), jnp.bfloat16),
             pltpu.VMEM((2, 3, 64) + unit, F32),
             pltpu.VMEM((3, 64) + unit, F32),
@@ -429,7 +464,15 @@
         ],
         compiler_params=pltpu.CompilerParams(collective_id=0, has_side_effects=True, vmem_limit_bytes=58 * 2**20),
         name="whitening",
-    )(projected, wide, scale)
+    )(projected, weight_exp, damp_exp)
+    return pl.pallas_call(
+        unpack_kernel,
+        out_shape=jax.ShapeDtypeStruct((8, HD, HD), F32),
+        in_specs=[pl.BlockSpec(memory_space=pltpu.VMEM)],
+        out_specs=pl.BlockSpec(memory_space=pl.ANY),
+        scratch_shapes=[pltpu.VMEM((8, HD, HD), F32), dma((8,))],
+        name="unpack",
+    )(pltpu.with_memory_space_constraint(packed, pltpu.VMEM))
 
 
 def solution(mesh):

time: 72.8 us -> 58.9 us (0.81)
  Pallas kernels: 67.2 us -> 58.6 us
  local copies, waits for them, and re-layouts: 3.42 us -> 0 us
  other arithmetic: 1.89 us -> 0 us
    pallas_call x1 -> x2, Pallas kernels: 67.2 us -> 58.6 us  [the longest x1 57.4 us: on_device(): pl.pallas_call(functools.partial(whitening_kernel, total), out_shape=OUT(...]
    unnamed x1 -> x0, local copies, waits for them, and re-layouts: 2.65 us -> none
    exp2 x1 -> x0, other arithmetic: 1.2 us -> none  [on_device(): scale = jnp.exp2(-damp_exp.astype(F32))]
    broadcast_in_dim x1 -> x0, local copies, waits for them, and re-layouts: 0.77 us -> none  [on_device(): wide = jnp.broadcast_to(weights[:, None], (weights.shape[0], 128))]
where the time goes in v2:
time: 58.9 us; the launch traced here: 58.6 us
  Pallas kernels  58.6 us (99%)
    pallas_call x1, Pallas kernels, on_device(): pl.pallas_call(functools.partial(whitening_kernel, total), out_shape=OUT(...  57.4 us
    pallas_call x1, Pallas kernels, on_device(): pl.pallas_call(unpack_kernel, out_shape=jax.ShapeDtypeStruct((8, HD, HD),...  1.27 us

profile of v2, /device:TPU:1, one launch (start us, length us, event | category | flops | bytes accessed | tf_op | source)
XLA Modules:
  0.0 58.6 jit_solution(3361726911147990655)
XLA Ops:
  0.0 57.4 %whitening.1.packed = f32[8,192,128]{2,1,0:T(8,128)S(1)} custom-call(bf16[384,24576]{1,0:T(8,128)(2,1)} %x_ref.1, s32[384]{0:T(512)} %weight_ref.1, s32[128]{0:T(128)} %damp_ref.1), custom_call_target="tpu_custom_call" | custom-call | tf_op jit(solution)/shard_map/whitening/pallas_call | solution.py:438
  57.4 1.3 %unpack.1 = f32[8,192,192]{2,1,0:T(8,128)} custom-call(f32[8,192,128]{2,1,0:T(8,128)S(1)} %whitening.1.packed), custom_call_target="tpu_custom_call" | custom-call | tf_op jit(solution)/shard_map/unpack/pallas_call | solution.py:468

commit v3 on v2

--- a/solution.py
+++ b/solution.py
@@ -9,7 +9,8 @@
 HD = 192
 ROWS = 56
 OUT = pltpu.VMEM
-LAG = 8
+LAG = 4
+LAG_X = 3
 MESH = pl.DeviceIdType.MESH
 F32 = jnp.float32
 
@@ -26,6 +27,15 @@
 
 def device(x, y, z, core):
     return (y % 2 * 4 + z, x * 4 + y // 2 * 2 + core)
+
+
+GROUPS = ((0, 0), (1, 0), (0, 1), (2, 0), (1, 1), (3, 0), (2, 1), (3, 1))
+
+
+def order(s):
+    xs = sum(x << (2 * i) for i, (x, _) in enumerate(GROUPS))
+    ys = sum(y << i for i, (_, y) in enumerate(GROUPS))
+    return lax.shift_right_logical(jnp.int32(xs), jnp.int32(2 * s)) % 4, lax.shift_right_logical(jnp.int32(ys), jnp.int32(s)) % 2
 
 
 def rel(step):
@@ -80,18 +90,29 @@
         cs = {(i, j): jnp.broadcast_to(m[i][:, 8 * k + j:8 * k + j + 1], (8, 128))
               for i in range(k, 8) for j in range(8)}
         diag = jnp.ones((8, 128), F32)
-        for j in range(8):
-            pivot = row(cs[k, j], j)
-            diag = jnp.where(sub == j, pivot, diag)
-            inv = 1.0 / pivot
-            scaled = row(m[k], j) * inv
-            below = jnp.where(sub > j, cs[k, j], 0.0)
-            us = {n: row(cs[k, n], j) * inv for n in range(j + 1, 8)}
+        for j in range(0, 8, 2):
+            a, b, e = row(cs[k, j], j), row(cs[k, j + 1], j), row(cs[k, j + 1], j + 1)
+            det = a * e - b * b
+            inv, over = 1.0 / det, 1.0 / a
+            ei, bi, ai = e * inv, b * inv, a * inv
+            r0, r1 = row(m[k], j), row(m[k], j + 1)
+            t0, t1 = ei * r0 - bi * r1, ai * r1 - bi * r0
+            below = sub > j + 1
+            second = jnp.where(sub == j + 1, b * over * r0, 0.0)
+            diag = jnp.where(sub == j, a, jnp.where(sub == j + 1, det * over, diag))
+            us = {}
+            for n in range(j + 2, 8):
+                c0, c1 = row(cs[k, n], j), row(cs[k, n], j + 1)
+                us[n] = (ei * c0 - bi * c1, ai * c1 - bi * c0)
             for i in range(k, 8):
-                f = below if i == k else cs[i, j]
-                m[i] = m[i] - f * scaled
-                for n in range(j + 1, 8):
-                    cs[i, n] = cs[i, n] - f * us[n]
+                f0, f1 = cs[i, j], cs[i, j + 1]
+                if i == k:
+                    f0, f1 = jnp.where(below, f0, 0.0), jnp.where(below, f1, 0.0)
+                    m[i] = m[i] - (f0 * t0 + f1 * t1 + second)
+                else:
+                    m[i] = m[i] - (f0 * t0 + f1 * t1)
+                for n in range(j + 2, 8):
+                    cs[i, n] = cs[i, n] - (f0 * us[n][0] + f1 * us[n][1])
         out.append((m[k] * lax.rsqrt(diag))[:, 64:])
     return jnp.concatenate(out, axis=0)
 
@@ -142,8 +163,8 @@
     emit(96, 96, jnp.concatenate([last, folded(w22)], axis=0))
 
 
-def whitening_kernel(total, x_ref, weight_ref, damp_ref, got, wexp, dexp, w_ref, esem, own, asem, bsem, xb, g, pr, rl, rr, fl, fr, f1, q2l, q2r, f2l, f2r, f2, f3, h,
-                  xsem, dsend, drecv, rsem, ssem, fsem, s2send, q2sem, f2sem, s3send, s3sem, hsem):
+def whitening_kernel(total, x_ref, weight_ref, damp_ref, got, wexp, dexp, w_ref, esem, own, asem, bsem, xb, g, pr, rl, rr, fl, fr, f1, q2, f2, f3, h,
+                  xsem, dsend, drecv, rsem, ssem, fsem, s2send, q2sem, s3send, s3sem, hsem):
     x, y, z, core = place()
     partner = device(x, y, z, 1 - core)
     right = (device((x + 1) % 4, y, z, core), device(x, (y + 1) % 4, z, core), device(x, y, (z + 1) % 4, core))
@@ -151,8 +172,9 @@
     far = (device((x + 2) % 4, y, z, core), device(x, (y + 2) % 4, z, core), device(x, y, (z + 2) % 4, core))
 
     def fetch(s, i):
-        px = (x + rel(s // 2)) % 4
-        py = (y + rel(s % 2 * 2 + i // 4)) % 4
+        xs, yh = order(s)
+        px = (x + rel(xs)) % 4
+        py = (y + rel(yh * 2 + i // 4)) % 4
         pz = (z + rel(i % 4)) % 4
         col = pl.multiple_of((px * 16 + py * 4 + pz) * 384, 384)
         return pltpu.make_async_copy(x_ref.at[:, pl.ds(col, 384)], xb.at[s % 2, i], xsem.at[s % 2, i])
@@ -182,9 +204,9 @@
         return pltpu.make_async_remote_copy(src_ref=src, dst_ref=dst, send_sem=send, recv_sem=recv,
                                             device_id=to, device_id_type=MESH)
 
-    def halves(s):
-        at = pl.ds(s * 8, 8)
-        return remote(g.at[1 - core, :, at], pr.at[:, at], dsend, drecv.at[s], partner)
+    def halves(s, part):
+        at = pl.ds(s * 8 + part * 4, 4)
+        return remote(g.at[1 - core, :, at], pr.at[:, at], dsend, drecv.at[s, part], partner)
 
     def mine(col, first, count):
         return g.at[core, col, pl.ds(first, count)]
@@ -195,11 +217,11 @@
     def to_left(col, src, dst, sem):
         remote(src, dst, ssem.at[col, 1], sem, left[col]).start()
 
-    def final_right(col, first, count, at):
-        to_right(col, mine(col, first, count), fl.at[col, pl.ds(at, count)], fsem.at[col, 0])
-
-    def final_left(col, first, count, at):
-        to_left(col, mine(col, first, count), fr.at[col, pl.ds(at, count)], fsem.at[col, 1])
+    def final_right(col, stage, first, count, at):
+        to_right(col, mine(col, first, count), fl.at[col, pl.ds(at, count)], fsem.at[col, 0, stage])
+
+    def final_left(col, stage, first, count, at):
+        to_left(col, mine(col, first, count), fr.at[col, pl.ds(at, count)], fsem.at[col, 1, stage])
 
     def relay_right(col, first, count, at, sem):
         to_right(col, mine(col, first, count), rl.at[col, pl.ds(at, count)], rsem.at[0, sem])
@@ -228,19 +250,22 @@
                 g[half, col, s * 8 + i, pl.ds(row, value.shape[0]), :] = value
 
             pack(low, high, put)
-
-        @pl.when(s == 0)
-        def _():
-            pl.semaphore_wait(barrier, len(peers))
-
-        halves(s).start()
+            if i == 3:
+                @pl.when(s == 0)
+                def _():
+                    pl.semaphore_wait(barrier, len(peers))
+
+                halves(s, 0).start()
+
+        halves(s, 1).start()
 
     def summed(s):
         base = s * 8
-        halves(s).wait_recv()
+        halves(s, 0).wait_recv()
+        halves(s, 1).wait_recv()
         for col in range(3):
             g[core, col, pl.ds(base, 8)] += pr[col, pl.ds(base, 8)]
-        xs, yh = s // 2, s % 2
+        xs, yh = order(s)
 
         @pl.when(xs == 0)
         def _():
@@ -249,55 +274,59 @@
 
         @pl.when(xs == 1)
         def _():
-            final_right(0, base + 4, 4, yh * 8 + 4)
+            final_right(0, 0, base + 4, 4, yh * 8 + 4)
 
         @pl.when(xs == 2)
         def _():
-            final_left(0, base, 4, yh * 8)
+            final_left(0, 0, base, 4, yh * 8)
 
         @pl.when(yh == 0)
         def _():
             relay_right(1, base, 2, xs * 2, 2 + xs)
             relay_left(1, base + 2, 2, xs * 2, 2 + xs)
-            final_right(1, base + 6, 2, xs * 4 + 2)
+            final_right(1, xs, base + 6, 2, xs * 4 + 2)
 
         @pl.when(yh == 1)
         def _():
-            final_left(1, base, 2, xs * 4)
+            final_left(1, xs, base, 2, xs * 4)
 
         relay_right(2, base, 1, s, 6 + s)
         relay_left(2, base + 4, 1, s, 6 + s)
-        final_right(2, base + 5, 1, s * 2 + 1)
-        final_left(2, base + 2, 1, s * 2)
-
-    def passed(s):
+        final_right(2, yh * (1 + xs // 2), base + 5, 1, yh * 8 + 4 + xs)
+        final_left(2, yh * (1 + xs // 2), base + 2, 1, yh * 8 + xs)
+
+    def passed_x(s):
         base = s * 8
-        xs, yh = s // 2, s % 2
+        xs, yh = order(s)
 
         @pl.when(xs == 1)
         def _():
             taken(rl, 0, 0, base, 4, yh * 4, yh)
-            final_right(0, base, 4, yh * 8)
+            final_right(0, 0, base, 4, yh * 8)
 
         @pl.when(xs == 2)
         def _():
             taken(rr, 1, 0, base + 4, 4, yh * 4, yh)
-            final_left(0, base + 4, 4, yh * 8 + 4)
+            final_left(0, 0, base + 4, 4, yh * 8 + 4)
+
+    def passed_yz(s):
+        base = s * 8
+        xs, yh = order(s)
 
         @pl.when(yh == 0)
         def _():
             taken(rl, 0, 1, base + 4, 2, xs * 2, 2 + xs)
-            final_right(1, base + 4, 2, xs * 4)
+            final_right(1, xs, base + 4, 2, xs * 4)
 
         @pl.when(yh == 1)
         def _():
             taken(rr, 1, 1, base + 2, 2, xs * 2, 2 + xs)
-            final_left(1, base + 2, 2, xs * 4 + 2)
+            final_left(1, xs, base + 2, 2, xs * 4 + 2)
 
         taken(rl, 0, 2, base + 1, 1, s, 6 + s)
-        final_right(2, base + 1, 1, s * 2)
+        final_right(2, yh * (1 + xs // 2), base + 1, 1, yh * 8 + xs)
         taken(rr, 1, 2, base + 6, 1, s, 6 + s)
-        final_left(2, base + 6, 1, s * 2 + 1)
+        final_left(2, yh * (1 + xs // 2), base + 6, 1, yh * 8 + 4 + xs)
 
     def step(s, carry):
         @pl.when(s < 7)
@@ -311,9 +340,13 @@
         def _():
             summed(s - 1)
 
+        @pl.when(s >= LAG_X)
+        def _():
+            passed_x(s - LAG_X)
+
         @pl.when(s >= LAG)
         def _():
-            passed(s - LAG)
+            passed_yz(s - LAG)
 
         return carry
 
@@ -321,44 +354,65 @@
     summed(7)
 
     def rest(s, carry):
-        passed(s)
+        pl.when(s >= 8 - LAG_X)(lambda: passed_x(s))
+        passed_yz(s)
         return carry
 
     lax.fori_loop(8 - LAG, 8, rest, 0)
 
-    axis2, axis3 = (1, 2, 0), (2, 0, 1)
+    axis2, axis3 = (2, 0, 1), (1, 2, 0)
+    hops = (far, right, left)
+
+    def arrived(col, stage, first, count):
+        for buf, side, to in ((fl, 0, left), (fr, 1, right)):
+            whole = buf.at[col, pl.ds(first, count)]
+            remote(whole, whole, ssem.at[col, side], fsem.at[col, side, stage], to[col]).wait_recv()
+
+    def complete(col, u, v):
+        group, i, at = (
+            ((3, v // 2), v % 2 * 4 + u, v * 4 + u),
+            ((u, 1), 4 + v, u * 4 + v),
+            ((v, u // 2), 3 + 4 * (u % 2), u * 4 + v),
+        )[col]
+        f1[col, u, v] = g[core, col, GROUPS.index(group) * 8 + i] + fl[col, at] + fr[col, at]
+
+    def second(col, u, first, count):
+        rows = pl.ds(first, count)
+        remote(f1.at[col, u, rows], q2.at[col, u, rows], s2send, q2sem.at[col, u], hops[u][axis2[col]]).start()
+
+    def along_x(u):
+        arrived(1, u, u * 4, 4)
+        for v in range(4):
+            complete(1, u, v)
+        if u < 3:
+            second(1, u, 0, 4)
+
+    arrived(0, 0, 0, 16)
+    for u in range(4):
+        for v in range(4):
+            complete(0, u, v)
+        if u < 3:
+            second(0, u, 0, 4)
+    along_x(0)
+    arrived(2, 0, 0, 8)
+    for u in range(2):
+        for v in range(4):
+            complete(2, u, v)
+        second(2, u, 0, 4)
+    along_x(1)
+    for k in range(2):
+        arrived(2, 1 + k, 8, 4)
+        for v in range(2 * k, 2 * k + 2):
+            for u in range(2, 4):
+                complete(2, u, v)
+        second(2, 2, 2 * k, 2)
+        along_x(2 + k)
     for col in range(3):
-        for buf, side, to in ((fl, 0, left), (fr, 1, right)):
-            remote(buf.at[col], buf.at[col], ssem.at[col, side], fsem.at[col, side], to[col]).wait_recv()
-        for a in range(4):
-            for b in range(4):
-                slot = (48 + a * 4 + b, (2 * a + 1) * 8 + 4 + b, (2 * a + b // 2) * 8 + 3 + 4 * (b % 2))[col]
-                at = b * 4 + a if col == 1 else a * 4 + b
-                f1[col, at] = g[core, col, slot] + fl[col, a * 4 + b] + fr[col, a * 4 + b]
-        ax = axis2[col]
-
-        def part(first):
-            return f1.at[col, pl.ds(first, 2)]
-
-        remote(part(0), q2l.at[col], s2send.at[col, 0], q2sem.at[col, 0], right[ax]).start()
-        remote(part(2), q2r.at[col], s2send.at[col, 1], q2sem.at[col, 1], left[ax]).start()
-        remote(part(6), f2l.at[col, pl.ds(2, 2)], s2send.at[col, 0], f2sem.at[col, 0], right[ax]).start()
-        remote(part(8), f2r.at[col, pl.ds(0, 2)], s2send.at[col, 1], f2sem.at[col, 1], left[ax]).start()
-    for col in range(3):
-        ax = axis2[col]
-        remote(q2l.at[col], q2l.at[col], s2send.at[col, 0], q2sem.at[col, 0], right[ax]).wait_recv()
-        f1[col, pl.ds(4, 2)] += q2l[col]
-        remote(f1.at[col, pl.ds(4, 2)], f2l.at[col, pl.ds(0, 2)], s2send.at[col, 0], f2sem.at[col, 0], right[ax]).start()
-        remote(q2r.at[col], q2r.at[col], s2send.at[col, 1], q2sem.at[col, 1], left[ax]).wait_recv()
-        f1[col, pl.ds(10, 2)] += q2r[col]
-        remote(f1.at[col, pl.ds(10, 2)], f2r.at[col, pl.ds(2, 2)], s2send.at[col, 1], f2sem.at[col, 1], left[ax]).start()
-    for col in range(3):
-        ax, ax3 = axis2[col], axis3[col]
-        remote(f2l.at[col], f2l.at[col], s2send.at[col, 0], f2sem.at[col, 0], right[ax]).wait_recv()
-        remote(f2r.at[col], f2r.at[col], s2send.at[col, 1], f2sem.at[col, 1], left[ax]).wait_recv()
-        f2[col] = f1[col, pl.ds(12, 4)] + f2l[col] + f2r[col]
-        for k, to in enumerate((far, right, left)):
-            remote(f2.at[col, k], f3.at[col, k], s3send.at[col, k], s3sem.at[col, k], to[ax3]).start()
+        for u in range(3):
+            remote(q2.at[col, u], q2.at[col, u], s2send, q2sem.at[col, u], right[col]).wait_recv()
+        f2[col] = (f1[col, 3] + q2[col, 0]) + (q2[col, 1] + q2[col, 2])
+        for k, to in enumerate(hops):
+            remote(f2.at[col, k], f3.at[col, k], s3send.at[col, k], s3sem.at[col, k], to[axis3[col]]).start()
     for col in range(3):
         for k, to in enumerate((far, right, left)):
             remote(f2.at[col, k], f3.at[col, k], s3send.at[col, k], s3sem.at[col, k], to[axis3[col]]).wait_recv()
@@ -398,13 +452,13 @@
     for col in range(3):
         for side in range(2):
             sent = g.at[core, col, pl.ds(0, 24)]
-            remote(sent, sent, ssem.at[col, side], fsem.at[col, side], right[col]).wait_send()
-            six = f1.at[col, pl.ds(0, 6)]
-            remote(six, six, s2send.at[col, side], f2sem.at[col, side], right[col]).wait_send()
+            remote(sent, sent, ssem.at[col, side], fsem.at[col, side, 0], right[col]).wait_send()
         for k in range(3):
             remote(f2.at[col, k], f3.at[col, k], s3send.at[col, k], s3sem.at[col, k], right[col]).wait_send()
+    ahead = g.at[core, 0, pl.ds(0, 36)]
+    remote(ahead, ahead, s2send, q2sem.at[0, 0], partner).wait_send()
     every = g.at[1 - core]
-    remote(every, pr, dsend, drecv.at[0], partner).wait_send()
+    remote(every, pr, dsend, drecv.at[0, 0], partner).wait_send()
     both.wait_send()
     seven = got.at[pl.ds(0, 7)]
     remote(seven, seven, asem, bsem.at[0], partner).wait_send()
@@ -451,16 +505,13 @@
             pltpu.VMEM((3, 8) + unit, F32),
             pltpu.VMEM((3, 16) + unit, F32),
             pltpu.VMEM((3, 16) + unit, F32),
-            pltpu.VMEM((3, 16) + unit, F32),
-            pltpu.VMEM((3, 2) + unit, F32),
-            pltpu.VMEM((3, 2) + unit, F32),
-            pltpu.VMEM((3, 4) + unit, F32),
-            pltpu.VMEM((3, 4) + unit, F32),
+            pltpu.VMEM((3, 4, 4) + unit, F32),
+            pltpu.VMEM((3, 3, 4) + unit, F32),
             pltpu.VMEM((3, 4) + unit, F32),
             pltpu.VMEM((3, 3) + unit, F32),
             pltpu.VMEM((2, 3) + unit, F32),
-            dma((2, 8)), dma, dma((8,)), dma((2, 14)), dma((3, 2)), dma((3, 2)),
-            dma((3, 2)), dma((3, 2)), dma((3, 2)), dma((3, 3)), dma((3, 3)), dma((2,)),
+            dma((2, 8)), dma, dma((8, 2)), dma((2, 14)), dma((3, 2)), dma((3, 2, 4)),
+            dma, dma((3, 3)), dma((3, 3)), dma((3, 3)), dma((2,)),
         ],
         compiler_params=pltpu.CompilerParams(collective_id=0, has_side_effects=True, vmem_limit_bytes=58 * 2**20),
         name="whitening",

time: 58.9 us -> 56.5 us (0.959)
  Pallas kernels: 58.6 us -> 56.2 us
    pallas_call x1, Pallas kernels: 57.4 us -> 54.9 us  [on_device(): pl.pallas_call(functools.partial(whitening_kernel, total), out_shape=OUT(...]
where the time goes in v3:
time: 56.5 us; the launch traced here: 56.2 us
  Pallas kernels  56.2 us (99%)
    pallas_call x1, Pallas kernels, on_device(): pl.pallas_call(functools.partial(whitening_kernel, total), out_shape=OUT(...  54.9 us
    pallas_call x1, Pallas kernels, on_device(): pl.pallas_call(unpack_kernel, out_shape=jax.ShapeDtypeStruct((8, HD, HD),...  1.27 us

profile of v3, /device:TPU:1, one launch (start us, length us, event | category | flops | bytes accessed | tf_op | source)
XLA Modules:
  0.0 56.2 jit_solution(8858881973925634974)
XLA Ops:
  0.0 54.9 %whitening.1.packed = f32[8,192,128]{2,1,0:T(8,128)S(1)} custom-call(bf16[384,24576]{1,0:T(8,128)(2,1)} %x_ref.1, s32[384]{0:T(512)} %weight_ref.1, s32[128]{0:T(128)} %damp_ref.1), custom_call_target="tpu_custom_call" | custom-call | tf_op jit(solution)/shard_map/whitening/pallas_call | solution.py:492
  54.9 1.3 %unpack.1 = f32[8,192,192]{2,1,0:T(8,128)} custom-call(f32[8,192,128]{2,1,0:T(8,128)S(1)} %whitening.1.packed), custom_call_target="tpu_custom_call" | custom-call | tf_op jit(solution)/shard_map/unpack/pallas_call | solution.py:519

commit v4 on v3

--- a/solution.py
+++ b/solution.py
@@ -8,9 +8,11 @@
 
 HD = 192
 ROWS = 56
+SIZE = (48, 56, 48)
+START = (0, 48, 104)
+HALF = 152
 OUT = pltpu.VMEM
 LAG = 4
-LAG_X = 3
 MESH = pl.DeviceIdType.MESH
 F32 = jnp.float32
 
@@ -29,7 +31,7 @@
     return (y % 2 * 4 + z, x * 4 + y // 2 * 2 + core)
 
 
-GROUPS = ((0, 0), (1, 0), (0, 1), (2, 0), (1, 1), (3, 0), (2, 1), (3, 1))
+GROUPS = ((0, 0), (0, 1), (1, 0), (2, 0), (1, 1), (3, 0), (2, 1), (3, 1))
 
 
 def order(s):
@@ -49,17 +51,21 @@
     left = c < 64
     a = jnp.where(r >= c, low[:128, :128], odd)
     b = jnp.where(left, low[:128, 128:], high[:, :128])
-    e = jnp.where(left[:64], low[128:192, 128:], low[192:, 128:])
+    top, turned = low[128:160, 128:], low[160:192, 128:]
+    upper, under = low[192:224, 128:], low[224:, 128:]
+    r32, c32 = r[:32], c[:32] % 64
+    e = jnp.where(left[:32], jnp.where(r32 >= c32, top, pltpu.roll(upper, 64, 1)),
+                  jnp.where(r32 + 32 >= c32, pltpu.roll(turned, 64, 1), under))
     d = jnp.sum(jnp.where(r == c, odd, 0.0), axis=0, keepdims=True)
-    put(0, 0, 0, a[:56])
-    put(0, 1, 0, a[56:112])
-    put(0, 2, 0, a[112:])
-    put(0, 2, 16, b[:40])
-    put(1, 0, 0, b[40:96])
-    put(1, 1, 0, b[96:])
-    put(1, 1, 32, e[:24])
-    put(1, 2, 0, e[24:])
-    put(1, 2, 40, jnp.broadcast_to(d, (16, 128)))
+    d2 = jnp.sum(jnp.where(r32 == c32, upper, 0.0) + jnp.where(r32 + 32 == c32, under, 0.0), axis=0, keepdims=True)
+    first = 0
+    for value in (a, b, e, jnp.where(r[:16] == 0, d, d2)):
+        while value.shape[0]:
+            half, at = divmod(first, HALF)
+            col = sum(at >= start for start in START) - 1
+            count = min(value.shape[0], START[col] + SIZE[col] - at)
+            put(half, col, at - START[col], value[:count])
+            value, first = value[count:], first + count
 
 
 def dot(a, b, ca, cb):
@@ -75,46 +81,44 @@
     return dot(a, b, 1, 1)
 
 
-def inverse_factor(d):
+def inverse_factor(d, width=16):
     r = lax.broadcasted_iota(jnp.int32, (64, 64), 0)
     c = lax.broadcasted_iota(jnp.int32, (64, 64), 1)
     full = jnp.concatenate([d, (r == c).astype(F32)], axis=1)
     m = [full[8 * i:8 * i + 8] for i in range(8)]
     sub = lax.broadcasted_iota(jnp.int32, (8, 128), 0)
-    out = []
+    diag = [jnp.ones((8, 128), F32) for _ in range(8)]
 
     def row(v, j):
         return jnp.broadcast_to(v[j:j + 1], (8, 128))
 
-    for k in range(8):
-        cs = {(i, j): jnp.broadcast_to(m[i][:, 8 * k + j:8 * k + j + 1], (8, 128))
-              for i in range(k, 8) for j in range(8)}
-        diag = jnp.ones((8, 128), F32)
-        for j in range(0, 8, 2):
-            a, b, e = row(cs[k, j], j), row(cs[k, j + 1], j), row(cs[k, j + 1], j + 1)
+    for base in range(0, 64, width):
+        cs = {(i, n): jnp.broadcast_to(m[i][:, n:n + 1], (8, 128))
+              for i in range(base // 8, 8) for n in range(base, base + width)}
+        for j in range(base, base + width, 2):
+            q, p = j // 8, j % 8
+            a, b, e = row(cs[q, j], p), row(cs[q, j + 1], p), row(cs[q, j + 1], p + 1)
             det = a * e - b * b
             inv, over = 1.0 / det, 1.0 / a
             ei, bi, ai = e * inv, b * inv, a * inv
-            r0, r1 = row(m[k], j), row(m[k], j + 1)
+            r0, r1 = row(m[q], p), row(m[q], p + 1)
             t0, t1 = ei * r0 - bi * r1, ai * r1 - bi * r0
-            below = sub > j + 1
-            second = jnp.where(sub == j + 1, b * over * r0, 0.0)
-            diag = jnp.where(sub == j, a, jnp.where(sub == j + 1, det * over, diag))
+            second = jnp.where(sub == p + 1, b * over * r0, 0.0)
+            diag[q] = jnp.where(sub == p, a, jnp.where(sub == p + 1, det * over, diag[q]))
             us = {}
-            for n in range(j + 2, 8):
-                c0, c1 = row(cs[k, n], j), row(cs[k, n], j + 1)
+            for n in range(j + 2, base + width):
+                c0, c1 = row(cs[q, n], p), row(cs[q, n], p + 1)
                 us[n] = (ei * c0 - bi * c1, ai * c1 - bi * c0)
-            for i in range(k, 8):
+            for i in range(q, 8):
                 f0, f1 = cs[i, j], cs[i, j + 1]
-                if i == k:
-                    f0, f1 = jnp.where(below, f0, 0.0), jnp.where(below, f1, 0.0)
+                if i == q:
+                    f0, f1 = jnp.where(sub > p + 1, f0, 0.0), jnp.where(sub > p + 1, f1, 0.0)
                     m[i] = m[i] - (f0 * t0 + f1 * t1 + second)
                 else:
                     m[i] = m[i] - (f0 * t0 + f1 * t1)
-                for n in range(j + 2, 8):
+                for n in range(j + 2, base + width):
                     cs[i, n] = cs[i, n] - (f0 * us[n][0] + f1 * us[n][1])
-        out.append((m[k] * lax.rsqrt(diag))[:, 64:])
-    return jnp.concatenate(out, axis=0)
+    return jnp.concatenate([(m[i] * lax.rsqrt(diag[i]))[:, 64:] for i in range(8)], axis=0)
 
 
 def folded(a):
@@ -125,13 +129,17 @@
     r = lax.broadcasted_iota(jnp.int32, (128, 128), 0)
     c = lax.broadcasted_iota(jnp.int32, (128, 128), 1)
     flat = flat / total
-    a, bc = flat[:128], flat[128:320]
+    a, b, e, lines = flat[:128], flat[128:256], flat[256:288], flat[288:296]
     t = a.T
     low = jnp.where(r >= c, a, t)
-    high = jnp.where(r < c, a, jnp.where(r == c, flat[320:321], t))
+    high = jnp.where(r < c, a, jnp.where(r == c, lines[0:1], t))
     a = jnp.where(even, low, high)
-    b = jnp.where(even, bc[:, :64], bc[:, 64:])
-    b0, b1, corner = b[:64], b[64:128], b[128:]
+    b = jnp.where(even, b[:, :64], b[:, 64:])
+    b0, b1 = b[:64], b[64:]
+    e = jnp.concatenate([e[:, :64], e[:, 64:]], axis=0)
+    rs, cc = r[:64, :64], c[:64, :64]
+    corner = jnp.where(even, jnp.where(rs >= cc, e, e.T),
+                       jnp.where(rs < cc, e, jnp.where(rs == cc, lines[1:2, 64:], e.T)))
     a00, a10, a11 = a[:64, :64], a[64:, :64], a[64:, 64:]
     g00 = jnp.where(even, a00, corner)
     g10 = jnp.where(even, a10, b0)
@@ -206,10 +214,11 @@
 
     def halves(s, part):
         at = pl.ds(s * 8 + part * 4, 4)
-        return remote(g.at[1 - core, :, at], pr.at[:, at], dsend, drecv.at[s, part], partner)
+        return [remote(g.at[1 - core, col, at, pl.ds(0, SIZE[col])], pr.at[col, at, pl.ds(0, SIZE[col])], dsend.at[col],
+                       drecv.at[s, part, col], partner) for col in range(3)]
 
     def mine(col, first, count):
-        return g.at[core, col, pl.ds(first, count)]
+        return g.at[core, col, pl.ds(first, count), pl.ds(0, SIZE[col])]
 
     def to_right(col, src, dst, sem):
         remote(src, dst, ssem.at[col, 0], sem, right[col]).start()
@@ -218,24 +227,25 @@
         remote(src, dst, ssem.at[col, 1], sem, left[col]).start()
 
     def final_right(col, stage, first, count, at):
-        to_right(col, mine(col, first, count), fl.at[col, pl.ds(at, count)], fsem.at[col, 0, stage])
+        to_right(col, mine(col, first, count), fl.at[col, pl.ds(at, count), pl.ds(0, SIZE[col])], fsem.at[col, 0, stage])
 
     def final_left(col, stage, first, count, at):
-        to_left(col, mine(col, first, count), fr.at[col, pl.ds(at, count)], fsem.at[col, 1, stage])
+        to_left(col, mine(col, first, count), fr.at[col, pl.ds(at, count), pl.ds(0, SIZE[col])], fsem.at[col, 1, stage])
 
     def relay_right(col, first, count, at, sem):
-        to_right(col, mine(col, first, count), rl.at[col, pl.ds(at, count)], rsem.at[0, sem])
+        to_right(col, mine(col, first, count), rl.at[col, pl.ds(at, count), pl.ds(0, SIZE[col])], rsem.at[0, sem])
 
     def relay_left(col, first, count, at, sem):
-        to_left(col, mine(col, first, count), rr.at[col, pl.ds(at, count)], rsem.at[1, sem])
+        to_left(col, mine(col, first, count), rr.at[col, pl.ds(at, count), pl.ds(0, SIZE[col])], rsem.at[1, sem])
 
     def taken(buf, side, col, first, count, at, sem):
-        part = buf.at[col, pl.ds(at, count)]
+        rows = pl.ds(0, SIZE[col])
+        part = buf.at[col, pl.ds(at, count), rows]
         remote(part, part, ssem.at[col, 0], rsem.at[side, sem], right[col]).wait_recv()
-        g[core, col, pl.ds(first, count)] += buf[col, pl.ds(at, count)]
+        g[core, col, pl.ds(first, count), rows] += buf[col, pl.ds(at, count), rows]
 
     def grams(s):
-        for i in range(8):
+        for i in range(4):
             fetch(s, i).wait()
 
         w = w_ref[...]
@@ -255,16 +265,20 @@
                 def _():
                     pl.semaphore_wait(barrier, len(peers))
 
-                halves(s, 0).start()
-
-        halves(s, 1).start()
+                for copy in halves(s, 0):
+                    copy.start()
+                for n in range(4, 8):
+                    fetch(s, n).wait()
+
+        for copy in halves(s, 1):
+            copy.start()
 
     def summed(s):
         base = s * 8
-        halves(s, 0).wait_recv()
-        halves(s, 1).wait_recv()
+        for copy in halves(s, 0) + halves(s, 1):
+            copy.wait_recv()
         for col in range(3):
-            g[core, col, pl.ds(base, 8)] += pr[col, pl.ds(base, 8)]
+            g[core, col, pl.ds(base, 8), pl.ds(0, SIZE[col])] += pr[col, pl.ds(base, 8), pl.ds(0, SIZE[col])]
         xs, yh = order(s)
 
         @pl.when(xs == 0)
@@ -274,11 +288,11 @@
 
         @pl.when(xs == 1)
         def _():
-            final_right(0, 0, base + 4, 4, yh * 8 + 4)
+            final_right(0, yh, base + 4, 4, yh * 8 + 4)
 
         @pl.when(xs == 2)
         def _():
-            final_left(0, 0, base, 4, yh * 8)
+            final_left(0, yh, base, 4, yh * 8)
 
         @pl.when(yh == 0)
         def _():
@@ -302,12 +316,12 @@
         @pl.when(xs == 1)
         def _():
             taken(rl, 0, 0, base, 4, yh * 4, yh)
-            final_right(0, 0, base, 4, yh * 8)
+            final_right(0, yh, base, 4, yh * 8)
 
         @pl.when(xs == 2)
         def _():
             taken(rr, 1, 0, base + 4, 4, yh * 4, yh)
-            final_left(0, 0, base + 4, 4, yh * 8 + 4)
+            final_left(0, yh, base + 4, 4, yh * 8 + 4)
 
     def passed_yz(s):
         base = s * 8
@@ -340,9 +354,18 @@
         def _():
             summed(s - 1)
 
-        @pl.when(s >= LAG_X)
-        def _():
-            passed_x(s - LAG_X)
+        @pl.when(s == 5)
+        def _():
+            passed_x(2)
+
+        @pl.when(s == 5)
+        def _():
+            passed_x(3)
+
+        @pl.when(s == 7)
+        def _():
+            passed_x(4)
+            passed_x(6)
 
         @pl.when(s >= LAG)
         def _():
@@ -354,7 +377,6 @@
     summed(7)
 
     def rest(s, carry):
-        pl.when(s >= 8 - LAG_X)(lambda: passed_x(s))
         passed_yz(s)
         return carry
 
@@ -365,7 +387,7 @@
 
     def arrived(col, stage, first, count):
         for buf, side, to in ((fl, 0, left), (fr, 1, right)):
-            whole = buf.at[col, pl.ds(first, count)]
+            whole = buf.at[col, pl.ds(first, count), pl.ds(0, SIZE[col])]
             remote(whole, whole, ssem.at[col, side], fsem.at[col, side, stage], to[col]).wait_recv()
 
     def complete(col, u, v):
@@ -374,11 +396,12 @@
             ((u, 1), 4 + v, u * 4 + v),
             ((v, u // 2), 3 + 4 * (u % 2), u * 4 + v),
         )[col]
-        f1[col, u, v] = g[core, col, GROUPS.index(group) * 8 + i] + fl[col, at] + fr[col, at]
+        rows = pl.ds(0, SIZE[col])
+        f1[col, u, v, rows] = g[core, col, GROUPS.index(group) * 8 + i, rows] + fl[col, at, rows] + fr[col, at, rows]
 
     def second(col, u, first, count):
-        rows = pl.ds(first, count)
-        remote(f1.at[col, u, rows], q2.at[col, u, rows], s2send, q2sem.at[col, u], hops[u][axis2[col]]).start()
+        part = (pl.ds(first, count), pl.ds(0, SIZE[col]))
+        remote(f1.at[(col, u) + part], q2.at[(col, u) + part], s2send.at[col], q2sem.at[col, u], hops[u][axis2[col]]).start()
 
     def along_x(u):
         arrived(1, u, u * 4, 4)
@@ -387,12 +410,15 @@
         if u < 3:
             second(1, u, 0, 4)
 
-    arrived(0, 0, 0, 16)
-    for u in range(4):
-        for v in range(4):
-            complete(0, u, v)
-        if u < 3:
-            second(0, u, 0, 4)
+    def along_z(half):
+        arrived(0, half, half * 8, 8)
+        for u in range(4):
+            for v in range(2 * half, 2 * half + 2):
+                complete(0, u, v)
+            if u < 3:
+                second(0, u, 2 * half, 2)
+
+    along_z(0)
     along_x(0)
     arrived(2, 0, 0, 8)
     for u in range(2):
@@ -400,6 +426,7 @@
             complete(2, u, v)
         second(2, u, 0, 4)
     along_x(1)
+    along_z(1)
     for k in range(2):
         arrived(2, 1 + k, 8, 4)
         for v in range(2 * k, 2 * k + 2):
@@ -407,20 +434,27 @@
                 complete(2, u, v)
         second(2, 2, 2 * k, 2)
         along_x(2 + k)
+    def third(col, k):
+        rows = pl.ds(0, SIZE[col])
+        return remote(f2.at[col, k, rows], f3.at[col, k, rows], s3send.at[col, k], s3sem.at[col, k], hops[k][axis3[col]])
+
     for col in range(3):
+        rows = pl.ds(0, SIZE[col])
         for u in range(3):
-            remote(q2.at[col, u], q2.at[col, u], s2send, q2sem.at[col, u], right[col]).wait_recv()
-        f2[col] = (f1[col, 3] + q2[col, 0]) + (q2[col, 1] + q2[col, 2])
-        for k, to in enumerate(hops):
-            remote(f2.at[col, k], f3.at[col, k], s3send.at[col, k], s3sem.at[col, k], to[axis3[col]]).start()
+            part = q2.at[col, u, :, rows]
+            remote(part, part, s2send.at[col], q2sem.at[col, u], right[col]).wait_recv()
+        f2[col, :, rows] = (f1[col, 3, :, rows] + q2[col, 0, :, rows]) + (q2[col, 1, :, rows] + q2[col, 2, :, rows])
+        for k in range(3):
+            third(col, k).start()
     for col in range(3):
-        for k, to in enumerate((far, right, left)):
-            remote(f2.at[col, k], f3.at[col, k], s3send.at[col, k], s3sem.at[col, k], to[axis3[col]]).wait_recv()
-        h[core, col] = (f2[col, 3] + f3[col, 0]) + (f3[col, 1] + f3[col, 2])
+        rows = pl.ds(0, SIZE[col])
+        for k in range(3):
+            third(col, k).wait_recv()
+        h[core, pl.ds(START[col], SIZE[col])] = (f2[col, 3, rows] + f3[col, 0, rows]) + (f3[col, 1, rows] + f3[col, 2, rows])
     both = remote(h.at[core], h.at[core], hsem.at[0], hsem.at[1], partner)
     both.start()
     both.wait_recv()
-    flat = jnp.concatenate([h[half, col] for half in range(2) for col in range(3)], axis=0)
+    flat = jnp.concatenate([h[0], h[1]], axis=0)
     owner = (x * 16 + y * 4 + z) * 2 + core
     lane = lax.broadcasted_iota(jnp.int32, (1, 128), 1)
     exponent = jnp.where(lane == owner, dexp[...].astype(F32).reshape(1, 128), 0.0)
@@ -451,14 +485,15 @@
 
     for col in range(3):
         for side in range(2):
-            sent = g.at[core, col, pl.ds(0, 24)]
+            sent = g.at[core, col, pl.ds(0, 24), pl.ds(0, SIZE[col])]
             remote(sent, sent, ssem.at[col, side], fsem.at[col, side, 0], right[col]).wait_send()
+        ahead = g.at[core, col, pl.ds(0, 12), pl.ds(0, SIZE[col])]
+        remote(ahead, ahead, s2send.at[col], q2sem.at[col, 0], right[col]).wait_send()
         for k in range(3):
-            remote(f2.at[col, k], f3.at[col, k], s3send.at[col, k], s3sem.at[col, k], right[col]).wait_send()
-    ahead = g.at[core, 0, pl.ds(0, 36)]
-    remote(ahead, ahead, s2send, q2sem.at[0, 0], partner).wait_send()
-    every = g.at[1 - core]
-    remote(every, pr, dsend, drecv.at[0, 0], partner).wait_send()
+            third(col, k).wait_send()
+    for col in range(3):
+        every = g.at[1 - core, col, :, pl.ds(0, SIZE[col])]
+        remote(every, every, dsend.at[col], drecv.at[0, 0, col], partner).wait_send()
     both.wait_send()
     seven = got.at[pl.ds(0, 7)]
     remote(seven, seven, asem, bsem.at[0], partner).wait_send()
@@ -509,9 +544,9 @@
             pltpu.VMEM((3, 3, 4) + unit, F32),
             pltpu.VMEM((3, 4) + unit, F32),
             pltpu.VMEM((3, 3) + unit, F32),
-            pltpu.VMEM((2, 3) + unit, F32),
-            dma((2, 8)), dma, dma((8, 2)), dma((2, 14)), dma((3, 2)), dma((3, 2, 4)),
-            dma, dma((3, 3)), dma((3, 3)), dma((3, 3)), dma((2,)),
+            pltpu.VMEM((2, 152, 128), F32),
+            dma((2, 8)), dma((3,)), dma((8, 2, 3)), dma((2, 14)), dma((3, 2)), dma((3, 2, 4)),
+            dma((3,)), dma((3, 3)), dma((3, 3)), dma((3, 3)), dma((2,)),
         ],
         compiler_params=pltpu.CompilerParams(collective_id=0, has_side_effects=True, vmem_limit_bytes=58 * 2**20),
         name="whitening",

time: 56.5 us -> 53.9 us (0.954)
  Pallas kernels: 56.2 us -> 53.8 us
    pallas_call x1, Pallas kernels: 54.9 us -> 52.5 us  [on_device(): pl.pallas_call(functools.partial(whitening_kernel, total), out_shape=OUT(...]
where the time goes in v4:
time: 53.9 us; the launch traced here: 53.8 us
  Pallas kernels  53.8 us (100%)
    pallas_call x1, Pallas kernels, on_device(): pl.pallas_call(functools.partial(whitening_kernel, total), out_shape=OUT(...  52.5 us
    pallas_call x1, Pallas kernels, on_device(): pl.pallas_call(unpack_kernel, out_shape=jax.ShapeDtypeStruct((8, HD, HD),...  1.27 us

profile of v4, /device:TPU:1, one launch (start us, length us, event | category | flops | bytes accessed | tf_op | source)
XLA Modules:
  0.0 53.8 jit_solution(8992539145874887518)
XLA Ops:
  0.0 52.5 %whitening.1.packed = f32[8,192,128]{2,1,0:T(8,128)S(1)} custom-call(bf16[384,24576]{1,0:T(8,128)(2,1)} %x_ref.1, s32[384]{0:T(512)} %weight_ref.1, s32[128]{0:T(128)} %damp_ref.1), custom_call_target="tpu_custom_call" | custom-call | tf_op jit(solution)/shard_map/whitening/pallas_call | solution.py:527
  52.5 1.3 %unpack.1 = f32[8,192,192]{2,1,0:T(8,128)} custom-call(f32[8,192,128]{2,1,0:T(8,128)S(1)} %whitening.1.packed), custom_call_target="tpu_custom_call" | custom-call | tf_op jit(solution)/shard_map/unpack/pallas_call | solution.py:554

commit v5 on v4

--- a/solution.py
+++ b/solution.py
@@ -167,8 +167,8 @@
     x21 = mul(l21, w11)
     x20 = x20 + mul(l21, w10)
     w22 = inverse_factor(s22)
-    last = jnp.concatenate([-mul(w22, x20), -mul(w22, x21)], axis=1)
-    emit(96, 96, jnp.concatenate([last, folded(w22)], axis=0))
+    emit(160, 32, folded(w22))
+    emit(96, 64, jnp.concatenate([-mul(w22, x20), -mul(w22, x21)], axis=1))
 
 
 def whitening_kernel(total, x_ref, weight_ref, damp_ref, got, wexp, dexp, w_ref, esem, own, asem, bsem, xb, g, pr, rl, rr, fl, fr, f1, q2, f2, f3, h,

time: 53.9 us -> 54.2 us (level)
  no operation moved by 1% of the time
where the time goes in v5:
time: 54.2 us; the launch traced here: 54.1 us
  Pallas kernels  54.1 us (100%)
    pallas_call x1, Pallas kernels, on_device(): pl.pallas_call(functools.partial(whitening_kernel, total), out_shape=OUT(...  52.8 us
    pallas_call x1, Pallas kernels, on_device(): pl.pallas_call(unpack_kernel, out_shape=jax.ShapeDtypeStruct((8, HD, HD),...  1.27 us

profile of v5, /device:TPU:1, one launch (start us, length us, event | category | flops | bytes accessed | tf_op | source)
XLA Modules:
  0.0 54.1 jit_solution(8398882291274631156)
XLA Ops:
  0.0 52.8 %whitening.1.packed = f32[8,192,128]{2,1,0:T(8,128)S(1)} custom-call(bf16[384,24576]{1,0:T(8,128)(2,1)} %x_ref.1, s32[384]{0:T(512)} %weight_ref.1, s32[128]{0:T(128)} %damp_ref.1), custom_call_target="tpu_custom_call" | custom-call | tf_op jit(solution)/shard_map/whitening/pallas_call | solution.py:527
  52.8 1.3 %unpack.1 = f32[8,192,192]{2,1,0:T(8,128)} custom-call(f32[8,192,128]{2,1,0:T(8,128)S(1)} %whitening.1.packed), custom_call_target="tpu_custom_call" | custom-call | tf_op jit(solution)/shard_map/unpack/pallas_call | solution.py:554
